TPU v7x, 32 devices: a whole 2x2x4 slice. The times are simulated.
32 devices in a mesh: radial: 8 (over z, x), phi: 4 (over y, core).
Axes of the slice: x: 2, y: 2, z: 4, core: 2. Of those that a mesh axis runs over, the one named last changes fastest.
Arguments:
- conserved: float32 [8, 64, 64, 128], P(None, 'radial', 'phi'), may hold values from -2.5 to 7, as said below
- core_mass: float32 [1], replicated, may hold values from 0.2 to 1
Outputs:
- advanced: float32 [8, 64, 64, 128], P(None, 'radial', 'phi')
- enclosed_mass: float32 [64], P('radial')
Inputs may be any that keep to these rules, and one draw needn't show every extreme that they name: conserved[0] (density) lies between 0.4 and 2.5; conserved[4] exceeds (conserved[1]^2 + conserved[2]^2 + conserved[3]^2)/(2 conserved[0]) by at least 0.6; the speeds |conserved[m]/conserved[0]| stay below 1; conserved[5..7] lie between 0 and conserved[0].
All inputs are finite; a program needn't handle non-finite values.
Results may differ from a plain program's by a relative error of at most 0.0003.
Values sent between devices are 32-bit elements; how exact they have to be, the bound alone decides.
A program may use at most 64 MiB of HBM per device.

v0:
```python
import math
import jax
import jax.numpy as jnp
from jax import lax
from jax.sharding import PartitionSpec as P

ADIABATIC = 4.0 / 3.0
INNER_RADIUS = 1.0
OUTER_RADIUS = 2.0
COURANT = 0.4
GRAVITY_KICK = 0.004
MINIMUM_DENSITY = 0.05
PRESSURE_FLOOR = 0.01


def entering(part, axis, combine, identity):
    place = lax.axis_index(axis)
    gathered = lax.all_gather(part, axis)
    state = jnp.zeros_like(part) + jnp.asarray(identity, part.dtype)

    def one(lap, state):
        return combine(state, lax.dynamic_index_in_dim(gathered, lap, 0, False))

    return lax.fori_loop(0, place, one, state)


def extended_2(value, sides, width, wrap):
    for axis, dim in sides:
        peers, length = (lax.axis_size(axis), value.shape[dim])
        up = [(i, (i + 1) % peers) for i in range(peers if wrap else peers - 1)]
        down = [(j, i) for i, j in up]
        last = lax.slice_in_dim(value, length - width, length, axis=dim)
        initial = lax.slice_in_dim(value, 0, width, axis=dim)
        before = lax.ppermute(last, axis, up)
        after = lax.ppermute(initial, axis, down)
        value = jnp.concatenate([before, value, after], axis=dim)
    return value


def step_sizes(radial_total, phi_total, theta_total):
    theta_step = math.pi / theta_total
    phi_step = 2.0 * math.pi / phi_total
    polar_width = INNER_RADIUS * math.sin(0.5 * theta_step) * phi_step
    radial_step = min(2.0 * polar_width, (OUTER_RADIUS - INNER_RADIUS) / radial_total)
    timestep = COURANT * min(radial_step, polar_width)
    return (radial_step, theta_step, phi_step, timestep)


def thermo(values):
    density = jnp.maximum(values[0], MINIMUM_DENSITY)
    kinetic = (
        0.5 * (values[1] * values[1] + values[2] * values[2] + values[3] * values[3]) / density
    )
    pressure = jnp.maximum((ADIABATIC - 1.0) * (values[4] - kinetic), PRESSURE_FLOOR * density)
    return (density, pressure)


def physical(values, component):
    density, pressure = thermo(values)
    normal = values[component] / density
    sound = jnp.sqrt(ADIABATIC * pressure / density)
    pieces = [values[which] * normal for which in range(values.shape[0])]
    pieces[component] = pieces[component] + pressure
    pieces[4] = pieces[4] + pressure * normal
    return (jnp.stack(pieces), jnp.abs(normal) + sound)


def face_flux(values, along_dim, component):
    interior = values.shape[along_dim] - 4
    neighbour_differences = lax.slice_in_dim(
        values, 1, interior + 4, axis=along_dim
    ) - lax.slice_in_dim(values, 0, interior + 3, axis=along_dim)
    below_diff = lax.slice_in_dim(neighbour_differences, 0, interior + 2, axis=along_dim)
    above_diff = lax.slice_in_dim(neighbour_differences, 1, interior + 3, axis=along_dim)
    limited = (
        0.5
        * (jnp.sign(below_diff) + jnp.sign(above_diff))
        * jnp.minimum(jnp.abs(below_diff), jnp.abs(above_diff))
    )
    left_state = lax.slice_in_dim(values, 1, interior + 2, axis=along_dim) + 0.5 * lax.slice_in_dim(
        limited, 0, interior + 1, axis=along_dim
    )
    right_state = lax.slice_in_dim(
        values, 2, interior + 3, axis=along_dim
    ) - 0.5 * lax.slice_in_dim(limited, 1, interior + 2, axis=along_dim)
    left_flux, left_signal = physical(left_state, component)
    right_flux, right_signal = physical(right_state, component)
    signal = jnp.maximum(left_signal, right_signal)
    return 0.5 * (left_flux + right_flux) - 0.5 * signal * (right_state - left_state)


def hydro_rate(extended, cell_centers, enclosed, radial_step, theta_step, phi_step, strength):
    theta_cells = extended.shape[3]
    centre_cells = extended[:, 2:-2, 2:-2, :]
    polar_padded = jnp.pad(centre_cells, ((0, 0), (0, 0), (0, 0), (2, 2)), mode="edge")
    radial_flux = face_flux(extended[:, :, 2:-2, :], 1, 1)
    polar_flux = face_flux(polar_padded, 3, 2)
    azimuth_flux = face_flux(extended[:, 2:-2, :, :], 2, 3)
    angles = (jnp.arange(theta_cells, dtype=jnp.float32) + 0.5) * theta_step
    sine_center = jnp.sin(angles)
    cosine = jnp.cos(angles)
    face_sine = jnp.sin(jnp.arange(theta_cells + 1, dtype=jnp.float32) * theta_step)
    radius = cell_centers[:, None, None]
    face_radius = jnp.concatenate(
        [cell_centers - 0.5 * radial_step, cell_centers[-1:] + 0.5 * radial_step]
    )[:, None, None]
    radial_area = face_radius * face_radius * radial_flux
    divergence = (radial_area[:, 1:] - radial_area[:, :-1]) / (radius * radius * radial_step)
    polar_area = face_sine * polar_flux
    divergence = divergence + (polar_area[..., 1:] - polar_area[..., :-1]) / (
        radius * sine_center * theta_step
    )
    divergence = divergence + (azimuth_flux[:, :, 1:] - azimuth_flux[:, :, :-1]) / (
        radius * sine_center * phi_step
    )
    density, pressure = thermo(centre_cells)
    radial_speed = centre_cells[1] / density
    polar_speed = centre_cells[2] / density
    azimuth_speed = centre_cells[3] / density
    cotangent = cosine / sine_center
    gravity_pull = strength * enclosed[:, None, None] / (radius * radius)
    source_radial = (
        2.0 * pressure + density * (polar_speed * polar_speed + azimuth_speed * azimuth_speed)
    ) / radius - density * gravity_pull
    source_polar = (
        pressure * cotangent
        + density * azimuth_speed * azimuth_speed * cotangent
        - density * radial_speed * polar_speed
    ) / radius
    source_azimuth = -density * azimuth_speed * (radial_speed + polar_speed * cotangent) / radius
    source_energy = -centre_cells[1] * gravity_pull
    nothing = jnp.zeros_like(pressure)
    source = jnp.stack(
        [
            nothing,
            source_radial,
            source_polar,
            source_azimuth,
            source_energy,
            nothing,
            nothing,
            nothing,
        ]
    )
    return source - divergence


def add_terms(earlier, later):
    return earlier + later


def body(conserved, core_mass):
    radial_rows = conserved.shape[1]
    phi_cells = conserved.shape[2]
    theta_cells = conserved.shape[3]
    radial_devices = lax.axis_size("radial")
    position = lax.axis_index("radial")
    radial_step, theta_step, phi_step, timestep = step_sizes(
        radial_rows * radial_devices, phi_cells * lax.axis_size("phi"), theta_cells
    )
    strength = GRAVITY_KICK / timestep
    first_row = position * radial_rows
    cell_centers = (
        INNER_RADIUS
        + ((first_row + jnp.arange(radial_rows, dtype=jnp.int32)).astype(jnp.float32) + 0.5)
        * radial_step
    )
    sine_center = jnp.sin((jnp.arange(theta_cells, dtype=jnp.float32) + 0.5) * theta_step)
    local_shells = jnp.dot(
        jnp.sum(conserved[0], axis=1), sine_center, precision=lax.Precision.HIGHEST
    )
    local_shells = (
        local_shells * cell_centers * cell_centers * (radial_step * theta_step * phi_step)
    )
    shells = lax.psum(local_shells, "phi")
    before = entering(jnp.sum(shells), "radial", add_terms, jnp.float32(0.0))
    enclosed = core_mass[0] + before + jnp.cumsum(shells) - 0.5 * shells

    def clipped_rows(extended, halo_width):
        total_rows = extended.shape[1]
        low_rows = jnp.where(
            position == 0,
            lax.slice_in_dim(extended, halo_width, halo_width + 1, axis=1),
            lax.slice_in_dim(extended, 0, halo_width, axis=1),
        )
        high_rows = jnp.where(
            position == radial_devices - 1,
            lax.slice_in_dim(
                extended, total_rows - halo_width - 1, total_rows - halo_width, axis=1
            ),
            lax.slice_in_dim(extended, total_rows - halo_width, total_rows, axis=1),
        )
        middle = lax.slice_in_dim(extended, halo_width, total_rows - halo_width, axis=1)
        return jnp.concatenate([low_rows, middle, high_rows], axis=1)

    def extend(values):
        wedge_split_state = extended_2(values, (("phi", 2),), 2, True)
        slab_split_state = extended_2(wedge_split_state, (("radial", 1),), 2, False)
        return clipped_rows(slab_split_state, 2)

    section_one = conserved + timestep * hydro_rate(
        extend(conserved), cell_centers, enclosed, radial_step, theta_step, phi_step, strength
    )
    section_two = section_one + timestep * hydro_rate(
        extend(section_one), cell_centers, enclosed, radial_step, theta_step, phi_step, strength
    )
    advanced = 0.5 * conserved + 0.5 * section_two
    return (advanced, enclosed)


def solution(mesh):
    in_specs = (P(None, "radial", "phi", None), P())
    out_specs = (P(None, "radial", "phi", None), P("radial"))
    return jax.shard_map(body, mesh=mesh, in_specs=in_specs, out_specs=out_specs, check_vma=False)
```

profile of v0, /device:TPU:24, one launch (start us, length us, event | category | flops | bytes accessed | tf_op | source)
XLA Modules:
  0.0 98.6 jit_solution(16917580335347414988)
XLA Ops:
  0.6 1.1 %fusion.53 = (f32[8,8,2,128]{3,2,1,0:T(2,128)S(1)}, f32[8,8,2,128]{3,2,1,0:T(2,128)S(1)}) fusion(f32[8,8,16,128]{3,2,1,0:T(8,128)} %param.4), kind=kLoop, calls=%fused_computation.338 | loop fusion | bytes 262144 | tf_op jit(solution)/shard_map/slice | solution.py:32
  1.8 0.6 copy.673
  2.4 0.6 copy.674
  3.0 1.7 %collective-permute-start.1 = (f32[8,8,2,128]{3,1,2,0:T(8,128)}, f32[8,8,2,128]{3,1,2,0:T(8,128)}, u32[]{:S(2)}, u32[]{:S(2)}) collective-permute-start(f32[8,8,2,128]{3,1,2,0:T(8,128)} %copy.674), channel_id=1, source_target_pairs={{1,0},{2,1},{3,2},{0,3},{5,4},{6,5},{7,6},{4,7},{9,8},{10,9},{11,1... | collective-permute-start | bytes 196616 | tf_op jit(solution)/shard_map/ppermute | solution.py:35
  4.8 0.6 multiply_multiply_fusion.4
  5.3 0.5 broadcast_add_fusion
  6.2 0.7 fusion.44
  6.9 0.6 constant_dynamic-update-slice_fusion.61
  9.6 0.7 minimum_multiply_fusion.1
  10.4 0.8 fusion.6
  11.8 0.8 copy-done.1
  12.6 1.0 copy-done.3
  13.6 0.7 fusion.2
  14.3 5.8 %psum.7 = f32[8]{0:T(128)S(1)} all-reduce(f32[8]{0:T(128)} %fusion.2), channel_id=1, replica_groups=mesh['radial'=8,'phi'=4] {'phi'}, use_global_device_ids=true, to_apply=%region_1.0 | all-reduce | flops 8 | bytes 64 | tf_op jit(solution)/shard_map/psum | solution.py:175
  20.0 0.6 reduce_sum.19
  20.6 1.3 %dynamic-slice = u32[1]{0:T(128)} dynamic-slice(u32[32]{0:T(128)} %constant.10, u32[]{:T(128)S(6)} %add.633), dynamic_slice_sizes={1} | dynamic-slice | bytes 12
  22.4 2.4 %dynamic-update-slice = f32[8]{0:T(128)} dynamic-update-slice(f32[8]{0:T(128)} %broadcast.552, f32[1]{0:T(128)} %bitcast.4, u32[]{:T(128)} %bitcast.5) | dynamic-update-slice | bytes 12
  24.8 0.6 slice.710
  25.4 17.5 %all-reduce = f32[8]{0:T(128)} all-reduce(f32[8]{0:T(128)} %dynamic-update-slice), channel_id=1, replica_groups=mesh['radial'=8,'phi'=4] {'radial'}, use_global_device_ids=true, to_apply=%add | all-reduce | flops 8 | bytes 64
  42.9 11.3 %while.10 = (s32[]{:T(128)}, f32[]{:T(128)}, s32[]{:T(128)}, f32[8]{0:T(128)}, s32[]{:T(128)}, /*index=5*/s32[]{:T(128)}, s32[]{:T(128)}) while((s32[]{:T(128)}, f32[]{:T(128)}, s32[]{:T(128)}, f32[8]{0:T(128)}, s32[]{:T(128)}, /*index=5*/s32[]{:T(128)}, s32[]{:T(128)}) %tuple.74), condition=%wide.region_4.5_spmd, body=%wide.region_3.4_spmd.sunk | while | flops 6 | bytes 135 | solution.py:24
  42.9 1.2 %dynamic_slice.5 = f32[1]{0:T(128)} dynamic-slice(f32[8]{0:T(128)} %get-tuple-element.163, s32[]{:T(128)S(6)} %select_n.41), dynamic_slice_sizes={1} | dynamic-slice | bytes 12 | tf_op jit(solution)/shard_map/while/body/jit(dynamic_index_in_dim)/dynamic_slice | solution.py:22
  44.8 1.2 %dynamic_slice.5 = f32[1]{0:T(128)} dynamic-slice(f32[8]{0:T(128)} %get-tuple-element.163, s32[]{:T(128)S(6)} %select_n.41), dynamic_slice_sizes={1} | dynamic-slice | bytes 12 | tf_op jit(solution)/shard_map/while/body/jit(dynamic_index_in_dim)/dynamic_slice | solution.py:22
  46.6 1.2 %dynamic_slice.5 = f32[1]{0:T(128)} dynamic-slice(f32[8]{0:T(128)} %get-tuple-element.163, s32[]{:T(128)S(6)} %select_n.41), dynamic_slice_sizes={1} | dynamic-slice | bytes 12 | tf_op jit(solution)/shard_map/while/body/jit(dynamic_index_in_dim)/dynamic_slice | solution.py:22
  48.5 1.2 %dynamic_slice.5 = f32[1]{0:T(128)} dynamic-slice(f32[8]{0:T(128)} %get-tuple-element.163, s32[]{:T(128)S(6)} %select_n.41), dynamic_slice_sizes={1} | dynamic-slice | bytes 12 | tf_op jit(solution)/shard_map/while/body/jit(dynamic_index_in_dim)/dynamic_slice | solution.py:22
  50.4 1.2 %dynamic_slice.5 = f32[1]{0:T(128)} dynamic-slice(f32[8]{0:T(128)} %get-tuple-element.163, s32[]{:T(128)S(6)} %select_n.41), dynamic_slice_sizes={1} | dynamic-slice | bytes 12 | tf_op jit(solution)/shard_map/while/body/jit(dynamic_index_in_dim)/dynamic_slice | solution.py:22
  52.3 1.2 %dynamic_slice.5 = f32[1]{0:T(128)} dynamic-slice(f32[8]{0:T(128)} %get-tuple-element.163, s32[]{:T(128)S(6)} %select_n.41), dynamic_slice_sizes={1} | dynamic-slice | bytes 12 | tf_op jit(solution)/shard_map/while/body/jit(dynamic_index_in_dim)/dynamic_slice | solution.py:22
  54.8 0.7 reduce-window.9
  55.5 1.2 %multiply_divide_fusion = (f32[8]{0:T(128)S(1)}, f32[8]{0:T(128)}) fusion(s32[]{:T(128)S(6)} %mul.1524, f32[8]{0:T(128)S(1)} %psum.7, f32[8,1]{0,1:T(1,128)} %reduce-window.9, f32[]{:T(128)S(6)} %add.521), kind=kLoop, calls=%fused_computation.325 | loop fusion | flops 88 | bytes 136 | tf_op jit(solution)/shard_map/div | solution.py:121
  57.1 0.8 multiply_multiply_fusion.3
  58.5 0.7 constant_dynamic-update-slice_fusion.23
  59.2 1.8 %subtract_multiply_fusion.1 = f32[8,8,16,129]{3,2,1,0:T(8,128)S(1)} fusion(f32[8,8,16,129]{3,2,1,0:T(8,128)S(1)} %get-tuple-element.87, f32[8,8,16,129]{3,2,1,0:T(8,128)S(1)} %get-tuple-element.86, f32[8,8,16,129]{3,2,1,0:T(8,128)} %get-tuple-element.116, f32[8,8,16,129]{3,2,1,0:T(8,128)S(1)} %get-tuple-element.117, f32[8,16,129]{2,1,0:T(8,128)S(1)} %get-tuple-element.70, ...), kind=kLoop, calls=%fused_computation.24 | loop fusion | flops 792576 | bytes 2708484 | tf_op jit(solution)/shard_map/mul | solution.py:109
  61.0 0.9 copy.630
  61.9 0.9 copy.631
  63.1 1.9 %collective-permute-start.3 = (f32[8,2,20,128]{3,0,2,1:T(8,128)S(1)}, f32[8,2,20,128]{3,0,2,1:T(8,128)S(1)}, u32[]{:S(2)}, u32[]{:S(2)}) collective-permute-start(f32[8,2,20,128]{3,0,2,1:T(8,128)S(1)} %copy.638), channel_id=1, source_target_pairs={{4,0},{8,4},{12,8},{16,12},{20,16},{24,20},{28,24},{5,1},{9,5},{13... | collective-permute-start | bytes 491528 | tf_op jit(solution)/shard_map/ppermute | solution.py:35
  65.1 4.7 %collective-permute-start.2 = (f32[8,2,20,128]{3,0,2,1:T(8,128)S(1)}, f32[8,2,20,128]{3,0,2,1:T(8,128)S(1)}, u32[]{:S(2)}, u32[]{:S(2)}) collective-permute-start(f32[8,2,20,128]{3,0,2,1:T(8,128)S(1)} %copy.634), channel_id=1, source_target_pairs={{0,4},{4,8},{8,12},{12,16},{16,20},{20,24},{24,28},{1,5},{5,9},{9,... | collective-permute-start | bytes 491528 | tf_op jit(solution)/shard_map/ppermute | solution.py:34
  69.8 0.6 minimum_multiply_fusion.3
  71.6 1.6 %collective-permute-done.2 = f32[8,2,20,128]{3,0,2,1:T(8,128)S(1)} collective-permute-done((f32[8,2,20,128]{3,0,2,1:T(8,128)S(1)}, f32[8,2,20,128]{3,0,2,1:T(8,128)S(1)}, u32[]{:S(2)}, u32[]{:S(2)}) %collective-permute-start.2) | collective-permute-done | bytes 163872 | tf_op jit(solution)/shard_map/ppermute | solution.py:34
  76.1 1.7 %collective-permute-start.5 = (f32[8,8,2,128]{3,1,2,0:T(8,128)S(1)}, f32[8,8,2,128]{3,1,2,0:T(8,128)S(1)}, u32[]{:S(2)}, u32[]{:S(2)}) collective-permute-start(f32[8,8,2,128]{3,1,2,0:T(8,128)S(1)} %copy.649), channel_id=1, source_target_pairs={{1,0},{2,1},{3,2},{0,3},{5,4},{6,5},{7,6},{4,7},{9,8},{10,9},{11,1... | collective-permute-start | bytes 196616 | tf_op jit(solution)/shard_map/ppermute | solution.py:35
  79.0 0.7 minimum_multiply_fusion
  79.8 0.8 fusion.4
  81.3 0.9 copy-done.4
  82.5 0.5 subtract_multiply_fusion
  83.5 3.8 %collective-permute-start.6 = (f32[8,2,20,128]{3,0,2,1:T(8,128)S(1)}, f32[8,2,20,128]{3,0,2,1:T(8,128)S(1)}, u32[]{:S(2)}, u32[]{:S(2)}) collective-permute-start(f32[8,2,20,128]{3,0,2,1:T(8,128)S(1)} %copy.654), channel_id=1, source_target_pairs={{0,4},{4,8},{8,12},{12,16},{16,20},{20,24},{24,28},{1,5},{5,9},{9,... | collective-permute-start | bytes 491528 | tf_op jit(solution)/shard_map/ppermute | solution.py:34
  87.4 2.9 %collective-permute-start.7 = (f32[8,2,20,128]{3,0,2,1:T(8,128)S(1)}, f32[8,2,20,128]{3,0,2,1:T(8,128)S(1)}, u32[]{:S(2)}, u32[]{:S(2)}) collective-permute-start(f32[8,2,20,128]{3,0,2,1:T(8,128)S(1)} %copy.658), channel_id=1, source_target_pairs={{4,0},{8,4},{12,8},{16,12},{20,16},{24,20},{28,24},{5,1},{9,5},{13... | collective-permute-start | bytes 491528 | tf_op jit(solution)/shard_map/ppermute | solution.py:35
  90.3 0.6 minimum_multiply_fusion.2
  92.0 0.6 collective-permute-done.6
  92.6 3.4 %collective-permute-done.7 = f32[8,2,20,128]{3,0,2,1:T(8,128)S(1)} collective-permute-done((f32[8,2,20,128]{3,0,2,1:T(8,128)S(1)}, f32[8,2,20,128]{3,0,2,1:T(8,128)S(1)}, u32[]{:S(2)}, u32[]{:S(2)}) %collective-permute-start.7) | collective-permute-done | bytes 163872 | tf_op jit(solution)/shard_map/ppermute | solution.py:35
  97.4 1.2 %fusion.32 = f32[8,8,16,128]{3,2,1,0:T(8,128)} fusion(f32[8,8,16,128]{3,2,1,0:T(8,128)S(1)} %copy-done, f32[8,8,16,128]{3,2,1,0:T(8,128)S(1)} %fusion.28, f32[8,8,16,128]{3,2,1,0:T(8,128)S(1)} %constant_dynamic-update-slice_fusion.55, f32[8,8,17,128]{3,2,1,0:T(8,128)S(1)} %multiply_subtract_fusion, f32[8,8,16,129]{3,2,1,0:T(8,128)S(1)} %subtract_multiply_fusion, ...), kind=kLoop, calls=%fused_computation.97 | loop fusion | flops 1703936 | bytes 5251104 | tf_op jit(solution)/shard_map/add | solution.py:207
  (182 shorter events, 12.9 us)
Async XLA Ops:
  0.6 5.2 %copy-start = (f32[8,8,16,128]{3,2,1,0:T(8,128)S(1)}, f32[8,8,16,128]{3,2,1,0:T(8,128)}, u32[]{:S(2)}) copy-start(f32[8,8,16,128]{3,2,1,0:T(8,128)} %param.4) | copy-start | bytes 1572868
  2.4 58.6 %collective-permute-start = (f32[8,8,2,128]{3,1,2,0:T(8,128)}, f32[8,8,2,128]{3,1,2,0:T(8,128)}, u32[]{:S(2)}, u32[]{:S(2)}) collective-permute-start(f32[8,8,2,128]{3,1,2,0:T(8,128)} %copy.673), channel_id=1, source_target_pairs={{0,1},{1,2},{2,3},{3,0},{4,5},{5,6},{6,7},{7,4},{8,9},{9,10},{10,1... | collective-permute-start | bytes 196616 | tf_op jit(solution)/shard_map/ppermute | solution.py:34
  3.0 58.9 %collective-permute-start.1 = (f32[8,8,2,128]{3,1,2,0:T(8,128)}, f32[8,8,2,128]{3,1,2,0:T(8,128)}, u32[]{:S(2)}, u32[]{:S(2)}) collective-permute-start(f32[8,8,2,128]{3,1,2,0:T(8,128)} %copy.674), channel_id=1, source_target_pairs={{1,0},{2,1},{3,2},{0,3},{5,4},{6,5},{7,6},{4,7},{9,8},{10,9},{11,1... | collective-permute-start | bytes 196616 | tf_op jit(solution)/shard_map/ppermute | solution.py:35
  11.6 1.0 copy-start.1
  12.6 1.0 %copy-start.3 = (f32[8,8,16,129]{3,2,1,0:T(8,128)}, f32[8,8,16,129]{3,2,1,0:T(8,128)S(1)}, u32[]{:S(2)}) copy-start(f32[8,8,16,129]{3,2,1,0:T(8,128)S(1)} %constant_dynamic-update-slice_fusion.24) | copy-start | bytes 1585156
  55.5 3.0 %copy-start.2 = (f32[8,8,16,129]{3,2,1,0:T(8,128)S(1)}, f32[8,8,16,129]{3,2,1,0:T(8,128)}, u32[]{:S(2)}) copy-start(f32[8,8,16,129]{3,2,1,0:T(8,128)} %copy-done.1) | copy-start | bytes 1585156
  59.2 1.8 %copy-start.6 = (f32[8]{0:T(128)S(1)}, f32[8]{0:T(128)}, u32[]{:S(2)}) copy-start(f32[8]{0:T(128)} %broadcast_add_fusion) | copy-start | bytes 100
  63.1 8.4 %collective-permute-start.3 = (f32[8,2,20,128]{3,0,2,1:T(8,128)S(1)}, f32[8,2,20,128]{3,0,2,1:T(8,128)S(1)}, u32[]{:S(2)}, u32[]{:S(2)}) collective-permute-start(f32[8,2,20,128]{3,0,2,1:T(8,128)S(1)} %copy.638), channel_id=1, source_target_pairs={{4,0},{8,4},{12,8},{16,12},{20,16},{24,20},{28,24},{5,1},{9,5},{13... | collective-permute-start | bytes 491528 | tf_op jit(solution)/shard_map/ppermute | solution.py:35
  65.1 8.1 %collective-permute-start.2 = (f32[8,2,20,128]{3,0,2,1:T(8,128)S(1)}, f32[8,2,20,128]{3,0,2,1:T(8,128)S(1)}, u32[]{:S(2)}, u32[]{:S(2)}) collective-permute-start(f32[8,2,20,128]{3,0,2,1:T(8,128)S(1)} %copy.634), channel_id=1, source_target_pairs={{0,4},{4,8},{8,12},{12,16},{16,20},{20,24},{24,28},{1,5},{5,9},{9,... | collective-permute-start | bytes 491528 | tf_op jit(solution)/shard_map/ppermute | solution.py:34
  74.4 0.7 copy-start.5
  76.0 7.1 %collective-permute-start.4 = (f32[8,8,2,128]{3,1,2,0:T(8,128)S(1)}, f32[8,8,2,128]{3,1,2,0:T(8,128)S(1)}, u32[]{:S(2)}, u32[]{:S(2)}) collective-permute-start(f32[8,8,2,128]{3,1,2,0:T(8,128)S(1)} %copy.648), channel_id=1, source_target_pairs={{0,1},{1,2},{2,3},{3,0},{4,5},{5,6},{6,7},{7,4},{8,9},{9,10},{10,1... | collective-permute-start | bytes 196616 | tf_op jit(solution)/shard_map/ppermute | solution.py:34
  76.1 7.0 %collective-permute-start.5 = (f32[8,8,2,128]{3,1,2,0:T(8,128)S(1)}, f32[8,8,2,128]{3,1,2,0:T(8,128)S(1)}, u32[]{:S(2)}, u32[]{:S(2)}) collective-permute-start(f32[8,8,2,128]{3,1,2,0:T(8,128)S(1)} %copy.649), channel_id=1, source_target_pairs={{1,0},{2,1},{3,2},{0,3},{5,4},{6,5},{7,6},{4,7},{9,8},{10,9},{11,1... | collective-permute-start | bytes 196616 | tf_op jit(solution)/shard_map/ppermute | solution.py:35
  81.1 1.0 %copy-start.4 = (f32[8,8,16,128]{3,2,1,0:T(8,128)S(1)}, f32[8,8,16,128]{3,2,1,0:T(8,128)}, u32[]{:S(2)}) copy-start(f32[8,8,16,128]{3,2,1,0:T(8,128)} %constant_dynamic-update-slice_fusion.61) | copy-start | bytes 1572868
  83.5 9.1 %collective-permute-start.6 = (f32[8,2,20,128]{3,0,2,1:T(8,128)S(1)}, f32[8,2,20,128]{3,0,2,1:T(8,128)S(1)}, u32[]{:S(2)}, u32[]{:S(2)}) collective-permute-start(f32[8,2,20,128]{3,0,2,1:T(8,128)S(1)} %copy.654), channel_id=1, source_target_pairs={{0,4},{4,8},{8,12},{12,16},{16,20},{20,24},{24,28},{1,5},{5,9},{9,... | collective-permute-start | bytes 491528 | tf_op jit(solution)/shard_map/ppermute | solution.py:34
  87.4 8.6 %collective-permute-start.7 = (f32[8,2,20,128]{3,0,2,1:T(8,128)S(1)}, f32[8,2,20,128]{3,0,2,1:T(8,128)S(1)}, u32[]{:S(2)}, u32[]{:S(2)}) collective-permute-start(f32[8,2,20,128]{3,0,2,1:T(8,128)S(1)} %copy.658), channel_id=1, source_target_pairs={{4,0},{8,4},{12,8},{16,12},{20,16},{24,20},{28,24},{5,1},{9,5},{13... | collective-permute-start | bytes 491528 | tf_op jit(solution)/shard_map/ppermute | solution.py:35
where the time goes:
time: 99.2 us; the launch traced here: 98.6 us
  blocking collectives  23.2 us (23%)
  local copies, waits for them, and re-layouts  22.9 us (23%)
  other arithmetic  22.4 us (23%)
  starting transfers between devices  16.9 us (17%)
  waiting for transfers between devices  5.66 us (6%)
  loops' own time  3.87 us (4%)
  between operations  3 us (3%)
    unnamed x1, blocking collectives  17.5 us
    unnamed x25, local copies, waits for them, and re-layouts  10.1 us
    ppermute x4, starting transfers between devices, extended_2(): before = lax.ppermute(last, axis, up)  8.58 us
    ppermute x4, starting transfers between devices, extended_2(): after = lax.ppermute(initial, axis, down)  8.32 us
    dynamic_slice x6, local copies, waits for them, and re-layouts, one(): return combine(state, lax.dynamic_index_in_dim(gathered, lap, 0, False))  7.39 us
    psum x1, blocking collectives, body(): shells = lax.psum(local_shells, 'phi')  5.76 us
    another operation x1, loops' own time, entering(): return lax.fori_loop(0, place, one, state)  3.87 us
    ppermute x4, waiting for transfers between devices, extended_2(): after = lax.ppermute(initial, axis, down)  3.39 us
  transfers between devices with their start and end apart: 8, of which 3 were waited for; matrix products, arithmetic and copies ran while one was open for 35% of the time, Pallas kernels for 0%

commit v1 on v0

--- a/solution.py
+++ b/solution.py
@@ -172,7 +172,7 @@
     local_shells = (
         local_shells * cell_centers * cell_centers * (radial_step * theta_step * phi_step)
     )
-    shells = lax.psum(local_shells, "phi")
+    shells = jnp.sum(lax.all_gather(local_shells, "phi"), axis=0)
     before = entering(jnp.sum(shells), "radial", add_terms, jnp.float32(0.0))
     enclosed = core_mass[0] + before + jnp.cumsum(shells) - 0.5 * shells
 

time: 99.2 us -> 99.4 us (level)
    psum x1 -> x0, blocking collectives: 5.76 us -> none  [body(): shells = lax.psum(local_shells, 'phi')]
    unnamed x1 -> x2, blocking collectives: 17.5 us -> 23.1 us
    unnamed x25 -> x32, local copies, waits for them, and re-layouts: 10.1 us -> 10.2 us
where the time goes in v1:
time: 99.4 us; the launch traced here: 98.8 us
  blocking collectives  23.1 us (23%)
  other arithmetic  23 us (23%)
  local copies, waits for them, and re-layouts  22.7 us (23%)
  starting transfers between devices  16.8 us (17%)
  waiting for transfers between devices  5.8 us (6%)
  between operations  3.87 us (4%)
  loops' own time  3.43 us (3%)
    unnamed x2, blocking collectives  23.1 us
    unnamed x32, local copies, waits for them, and re-layouts  10.2 us
    ppermute x4, starting transfers between devices, extended_2(): after = lax.ppermute(initial, axis, down)  8.46 us
    ppermute x4, starting transfers between devices, extended_2(): before = lax.ppermute(last, axis, up)  8.3 us
    dynamic_slice x6, local copies, waits for them, and re-layouts, one(): return combine(state, lax.dynamic_index_in_dim(gathered, lap, 0, False))  6.97 us
    another operation x1, loops' own time, entering(): return lax.fori_loop(0, place, one, state)  3.43 us
    ppermute x4, waiting for transfers between devices, extended_2(): after = lax.ppermute(initial, axis, down)  3.38 us
    mul x6, other arithmetic, face_flux(): 0.5 * (jnp.sign(below_diff) + jnp.sign(above_diff))  3.14 us
  transfers between devices with their start and end apart: 8, of which 3 were waited for; matrix products, arithmetic and copies ran while one was open for 35% of the time, Pallas kernels for 0%

profile of v1, /device:TPU:24, one launch (start us, length us, event | category | flops | bytes accessed | tf_op | source)
XLA Modules:
  0.0 98.8 jit_solution(5330379107083946815)
XLA Ops:
  0.6 1.1 %fusion.53 = (f32[8,8,2,128]{3,2,1,0:T(2,128)S(1)}, f32[8,8,2,128]{3,2,1,0:T(2,128)S(1)}) fusion(f32[8,8,16,128]{3,2,1,0:T(8,128)} %param.4), kind=kLoop, calls=%fused_computation.338 | loop fusion | bytes 262144 | tf_op jit(solution)/shard_map/slice | solution.py:32
  1.8 0.6 copy.673
  2.4 0.6 copy.674
  3.0 1.7 %collective-permute-start.1 = (f32[8,8,2,128]{3,1,2,0:T(8,128)}, f32[8,8,2,128]{3,1,2,0:T(8,128)}, u32[]{:S(2)}, u32[]{:S(2)}) collective-permute-start(f32[8,8,2,128]{3,1,2,0:T(8,128)} %copy.674), channel_id=1, source_target_pairs={{1,0},{2,1},{3,2},{0,3},{5,4},{6,5},{7,6},{4,7},{9,8},{10,9},{11,1... | collective-permute-start | bytes 196616 | tf_op jit(solution)/shard_map/ppermute | solution.py:35
  4.8 0.6 multiply_multiply_fusion.4
  5.4 0.6 broadcast_add_fusion
  6.4 0.6 dynamic-slice
  7.9 5.6 %all-reduce = f32[32]{0:T(128)S(1)} all-reduce(f32[32]{0:T(128)S(1)} %dynamic-update-slice), channel_id=2, replica_groups=mesh['radial'=8,'phi'=4] {'phi'}, use_global_device_ids=true, to_apply=%add | all-reduce | flops 32 | bytes 256
  13.5 0.7 reduce_sum.28
  14.4 0.6 fusion.44
  14.9 0.6 constant_dynamic-update-slice_fusion.61
  17.7 0.7 minimum_multiply_fusion.1
  18.4 0.8 fusion.6
  19.9 0.8 copy-done.1
  20.7 1.0 %copy-done.3 = f32[8,8,16,129]{3,2,1,0:T(8,128)} copy-done((f32[8,8,16,129]{3,2,1,0:T(8,128)}, f32[8,8,16,129]{3,2,1,0:T(8,128)S(1)}, u32[]{:S(2)}) %copy-start.3) | copy-done | bytes 528408
  21.6 0.6 dynamic-slice.1
  22.7 2.4 %dynamic-update-slice.1 = f32[8]{0:T(128)} dynamic-update-slice(f32[8]{0:T(128)} %broadcast.580, f32[1]{0:T(128)} %bitcast.5, u32[]{:T(128)} %bitcast.6) | dynamic-update-slice | bytes 12
  25.1 0.7 slice.710
  25.8 17.4 %all-reduce.1 = f32[8]{0:T(128)} all-reduce(f32[8]{0:T(128)} %dynamic-update-slice.1), channel_id=1, replica_groups=mesh['radial'=8,'phi'=4] {'radial'}, use_global_device_ids=true, to_apply=%add.1 | all-reduce | flops 8 | bytes 64
  43.2 10.4 %while.10 = (s32[]{:T(128)}, f32[]{:T(128)}, s32[]{:T(128)}, f32[8]{0:T(128)}, s32[]{:T(128)}, /*index=5*/s32[]{:T(128)}, s32[]{:T(128)}) while((s32[]{:T(128)}, f32[]{:T(128)}, s32[]{:T(128)}, f32[8]{0:T(128)}, s32[]{:T(128)}, /*index=5*/s32[]{:T(128)}, s32[]{:T(128)}) %tuple.74), condition=%wide.region_3.4_spmd, body=%wide.region_2.0_spmd.sunk | while | flops 6 | bytes 135 | solution.py:24
  43.2 1.2 %dynamic_slice.5 = f32[1]{0:T(128)} dynamic-slice(f32[8]{0:T(128)} %get-tuple-element.163, s32[]{:T(128)S(6)} %select_n.41), dynamic_slice_sizes={1} | dynamic-slice | bytes 12 | tf_op jit(solution)/shard_map/while/body/jit(dynamic_index_in_dim)/dynamic_slice | solution.py:22
  44.9 1.2 %dynamic_slice.5 = f32[1]{0:T(128)} dynamic-slice(f32[8]{0:T(128)} %get-tuple-element.163, s32[]{:T(128)S(6)} %select_n.41), dynamic_slice_sizes={1} | dynamic-slice | bytes 12 | tf_op jit(solution)/shard_map/while/body/jit(dynamic_index_in_dim)/dynamic_slice | solution.py:22
  46.7 1.2 %dynamic_slice.5 = f32[1]{0:T(128)} dynamic-slice(f32[8]{0:T(128)} %get-tuple-element.163, s32[]{:T(128)S(6)} %select_n.41), dynamic_slice_sizes={1} | dynamic-slice | bytes 12 | tf_op jit(solution)/shard_map/while/body/jit(dynamic_index_in_dim)/dynamic_slice | solution.py:22
  48.4 1.2 %dynamic_slice.5 = f32[1]{0:T(128)} dynamic-slice(f32[8]{0:T(128)} %get-tuple-element.163, s32[]{:T(128)S(6)} %select_n.41), dynamic_slice_sizes={1} | dynamic-slice | bytes 12 | tf_op jit(solution)/shard_map/while/body/jit(dynamic_index_in_dim)/dynamic_slice | solution.py:22
  50.2 1.2 %dynamic_slice.5 = f32[1]{0:T(128)} dynamic-slice(f32[8]{0:T(128)} %get-tuple-element.163, s32[]{:T(128)S(6)} %select_n.41), dynamic_slice_sizes={1} | dynamic-slice | bytes 12 | tf_op jit(solution)/shard_map/while/body/jit(dynamic_index_in_dim)/dynamic_slice | solution.py:22
  51.9 1.2 %dynamic_slice.5 = f32[1]{0:T(128)} dynamic-slice(f32[8]{0:T(128)} %get-tuple-element.163, s32[]{:T(128)S(6)} %select_n.41), dynamic_slice_sizes={1} | dynamic-slice | bytes 12 | tf_op jit(solution)/shard_map/while/body/jit(dynamic_index_in_dim)/dynamic_slice | solution.py:22
  54.3 0.5 reduce_sum.29
  54.8 0.8 reduce-window.7
  55.6 1.3 %multiply_divide_fusion = (f32[8]{0:T(128)S(1)}, f32[8]{0:T(128)}) fusion(s32[]{:T(128)S(6)} %mul.1540, f32[8]{0:T(128)} %reduce_sum.29, f32[8,1]{0,1:T(1,128)S(1)} %reduce-window.7, f32[]{:T(128)S(6)} %add.535), kind=kLoop, calls=%fused_computation.325 | loop fusion | flops 88 | bytes 136 | tf_op jit(solution)/shard_map/div | solution.py:121
  57.3 0.7 multiply_multiply_fusion.3
  58.6 0.7 constant_dynamic-update-slice_fusion.23
  59.3 1.8 %subtract_multiply_fusion.1 = f32[8,8,16,129]{3,2,1,0:T(8,128)S(1)} fusion(f32[8,8,16,129]{3,2,1,0:T(8,128)S(1)} %get-tuple-element.87, f32[8,8,16,129]{3,2,1,0:T(8,128)S(1)} %get-tuple-element.86, f32[8,8,16,129]{3,2,1,0:T(8,128)} %get-tuple-element.116, f32[8,8,16,129]{3,2,1,0:T(8,128)S(1)} %get-tuple-element.117, f32[8,16,129]{2,1,0:T(8,128)S(1)} %get-tuple-element.70, ...), kind=kLoop, calls=%fused_computation.24 | loop fusion | flops 792576 | bytes 2708484 | tf_op jit(solution)/shard_map/mul | solution.py:109
  61.2 0.9 copy.630
  62.1 0.9 copy.631
  63.3 1.9 %collective-permute-start.3 = (f32[8,2,20,128]{3,0,2,1:T(8,128)S(1)}, f32[8,2,20,128]{3,0,2,1:T(8,128)S(1)}, u32[]{:S(2)}, u32[]{:S(2)}) collective-permute-start(f32[8,2,20,128]{3,0,2,1:T(8,128)S(1)} %copy.638), channel_id=1, source_target_pairs={{4,0},{8,4},{12,8},{16,12},{20,16},{24,20},{28,24},{5,1},{9,5},{13... | collective-permute-start | bytes 491528 | tf_op jit(solution)/shard_map/ppermute | solution.py:35
  65.3 4.6 %collective-permute-start.2 = (f32[8,2,20,128]{3,0,2,1:T(8,128)S(1)}, f32[8,2,20,128]{3,0,2,1:T(8,128)S(1)}, u32[]{:S(2)}, u32[]{:S(2)}) collective-permute-start(f32[8,2,20,128]{3,0,2,1:T(8,128)S(1)} %copy.634), channel_id=1, source_target_pairs={{0,4},{4,8},{8,12},{12,16},{16,20},{20,24},{24,28},{1,5},{5,9},{9,... | collective-permute-start | bytes 491528 | tf_op jit(solution)/shard_map/ppermute | solution.py:34
  69.8 0.6 minimum_multiply_fusion.3
  71.5 1.8 %collective-permute-done.2 = f32[8,2,20,128]{3,0,2,1:T(8,128)S(1)} collective-permute-done((f32[8,2,20,128]{3,0,2,1:T(8,128)S(1)}, f32[8,2,20,128]{3,0,2,1:T(8,128)S(1)}, u32[]{:S(2)}, u32[]{:S(2)}) %collective-permute-start.2) | collective-permute-done | bytes 163872 | tf_op jit(solution)/shard_map/ppermute | solution.py:34
  76.3 1.7 %collective-permute-start.5 = (f32[8,8,2,128]{3,1,2,0:T(8,128)S(1)}, f32[8,8,2,128]{3,1,2,0:T(8,128)S(1)}, u32[]{:S(2)}, u32[]{:S(2)}) collective-permute-start(f32[8,8,2,128]{3,1,2,0:T(8,128)S(1)} %copy.649), channel_id=1, source_target_pairs={{1,0},{2,1},{3,2},{0,3},{5,4},{6,5},{7,6},{4,7},{9,8},{10,9},{11,1... | collective-permute-start | bytes 196616 | tf_op jit(solution)/shard_map/ppermute | solution.py:35
  79.2 0.7 minimum_multiply_fusion
  79.9 0.7 fusion.4
  81.4 0.9 copy-done.4
  83.7 3.7 %collective-permute-start.6 = (f32[8,2,20,128]{3,0,2,1:T(8,128)S(1)}, f32[8,2,20,128]{3,0,2,1:T(8,128)S(1)}, u32[]{:S(2)}, u32[]{:S(2)}) collective-permute-start(f32[8,2,20,128]{3,0,2,1:T(8,128)S(1)} %copy.654), channel_id=1, source_target_pairs={{0,4},{4,8},{8,12},{12,16},{16,20},{20,24},{24,28},{1,5},{5,9},{9,... | collective-permute-start | bytes 491528 | tf_op jit(solution)/shard_map/ppermute | solution.py:34
  87.4 3.1 %collective-permute-start.7 = (f32[8,2,20,128]{3,0,2,1:T(8,128)S(1)}, f32[8,2,20,128]{3,0,2,1:T(8,128)S(1)}, u32[]{:S(2)}, u32[]{:S(2)}) collective-permute-start(f32[8,2,20,128]{3,0,2,1:T(8,128)S(1)} %copy.658), channel_id=1, source_target_pairs={{4,0},{8,4},{12,8},{16,12},{20,16},{24,20},{28,24},{5,1},{9,5},{13... | collective-permute-start | bytes 491528 | tf_op jit(solution)/shard_map/ppermute | solution.py:35
  90.5 0.6 minimum_multiply_fusion.2
  92.2 0.6 collective-permute-done.6
  92.8 3.4 %collective-permute-done.7 = f32[8,2,20,128]{3,0,2,1:T(8,128)S(1)} collective-permute-done((f32[8,2,20,128]{3,0,2,1:T(8,128)S(1)}, f32[8,2,20,128]{3,0,2,1:T(8,128)S(1)}, u32[]{:S(2)}, u32[]{:S(2)}) %collective-permute-start.7) | collective-permute-done | bytes 163872 | tf_op jit(solution)/shard_map/ppermute | solution.py:35
  97.5 1.2 %fusion.32 = f32[8,8,16,128]{3,2,1,0:T(8,128)} fusion(f32[8,8,16,128]{3,2,1,0:T(8,128)S(1)} %copy-done, f32[8,8,16,128]{3,2,1,0:T(8,128)S(1)} %fusion.28, f32[8,8,16,128]{3,2,1,0:T(8,128)S(1)} %constant_dynamic-update-slice_fusion.55, f32[8,8,17,128]{3,2,1,0:T(8,128)S(1)} %multiply_subtract_fusion, f32[8,8,16,129]{3,2,1,0:T(8,128)S(1)} %subtract_multiply_fusion, ...), kind=kLoop, calls=%fused_computation.97 | loop fusion | flops 1703936 | bytes 5251104 | tf_op jit(solution)/shard_map/add | solution.py:207
  (191 shorter events, 13.8 us)
Async XLA Ops:
  0.6 5.3 %copy-start = (f32[8,8,16,128]{3,2,1,0:T(8,128)S(1)}, f32[8,8,16,128]{3,2,1,0:T(8,128)}, u32[]{:S(2)}) copy-start(f32[8,8,16,128]{3,2,1,0:T(8,128)} %param.4) | copy-start | bytes 1572868
  2.4 4.0 %copy-start.8 = (u32[32]{0:T(128)S(1)}, u32[32]{0:T(128)}, u32[]{:S(2)}) copy-start(u32[32]{0:T(128)} %constant.10) | copy-start | bytes 388
  2.4 58.8 %collective-permute-start = (f32[8,8,2,128]{3,1,2,0:T(8,128)}, f32[8,8,2,128]{3,1,2,0:T(8,128)}, u32[]{:S(2)}, u32[]{:S(2)}) collective-permute-start(f32[8,8,2,128]{3,1,2,0:T(8,128)} %copy.673), channel_id=1, source_target_pairs={{0,1},{1,2},{2,3},{3,0},{4,5},{5,6},{6,7},{7,4},{8,9},{9,10},{10,1... | collective-permute-start | bytes 196616 | tf_op jit(solution)/shard_map/ppermute | solution.py:34
  3.0 59.0 %collective-permute-start.1 = (f32[8,8,2,128]{3,1,2,0:T(8,128)}, f32[8,8,2,128]{3,1,2,0:T(8,128)}, u32[]{:S(2)}, u32[]{:S(2)}) collective-permute-start(f32[8,8,2,128]{3,1,2,0:T(8,128)} %copy.674), channel_id=1, source_target_pairs={{1,0},{2,1},{3,2},{0,3},{5,4},{6,5},{7,6},{4,7},{9,8},{10,9},{11,1... | collective-permute-start | bytes 196616 | tf_op jit(solution)/shard_map/ppermute | solution.py:35
  19.6 1.0 copy-start.1
  19.7 1.9 %copy-start.7 = (u32[32]{0:T(128)S(1)}, u32[32]{0:T(128)}, u32[]{:S(2)}) copy-start(u32[32]{0:T(128)} %constant.15) | copy-start | bytes 388
  20.6 1.0 %copy-start.3 = (f32[8,8,16,129]{3,2,1,0:T(8,128)}, f32[8,8,16,129]{3,2,1,0:T(8,128)S(1)}, u32[]{:S(2)}) copy-start(f32[8,8,16,129]{3,2,1,0:T(8,128)S(1)} %constant_dynamic-update-slice_fusion.24) | copy-start | bytes 1585156
  55.6 3.0 %copy-start.2 = (f32[8,8,16,129]{3,2,1,0:T(8,128)S(1)}, f32[8,8,16,129]{3,2,1,0:T(8,128)}, u32[]{:S(2)}) copy-start(f32[8,8,16,129]{3,2,1,0:T(8,128)} %copy-done.1) | copy-start | bytes 1585156
  59.3 1.8 %copy-start.6 = (f32[8]{0:T(128)S(1)}, f32[8]{0:T(128)}, u32[]{:S(2)}) copy-start(f32[8]{0:T(128)} %broadcast_add_fusion) | copy-start | bytes 100
  63.3 8.2 %collective-permute-start.3 = (f32[8,2,20,128]{3,0,2,1:T(8,128)S(1)}, f32[8,2,20,128]{3,0,2,1:T(8,128)S(1)}, u32[]{:S(2)}, u32[]{:S(2)}) collective-permute-start(f32[8,2,20,128]{3,0,2,1:T(8,128)S(1)} %copy.638), channel_id=1, source_target_pairs={{4,0},{8,4},{12,8},{16,12},{20,16},{24,20},{28,24},{5,1},{9,5},{13... | collective-permute-start | bytes 491528 | tf_op jit(solution)/shard_map/ppermute | solution.py:35
  65.3 8.1 %collective-permute-start.2 = (f32[8,2,20,128]{3,0,2,1:T(8,128)S(1)}, f32[8,2,20,128]{3,0,2,1:T(8,128)S(1)}, u32[]{:S(2)}, u32[]{:S(2)}) collective-permute-start(f32[8,2,20,128]{3,0,2,1:T(8,128)S(1)} %copy.634), channel_id=1, source_target_pairs={{0,4},{4,8},{8,12},{12,16},{16,20},{20,24},{24,28},{1,5},{5,9},{9,... | collective-permute-start | bytes 491528 | tf_op jit(solution)/shard_map/ppermute | solution.py:34
  74.6 0.7 copy-start.5
  76.2 7.0 %collective-permute-start.4 = (f32[8,8,2,128]{3,1,2,0:T(8,128)S(1)}, f32[8,8,2,128]{3,1,2,0:T(8,128)S(1)}, u32[]{:S(2)}, u32[]{:S(2)}) collective-permute-start(f32[8,8,2,128]{3,1,2,0:T(8,128)S(1)} %copy.648), channel_id=1, source_target_pairs={{0,1},{1,2},{2,3},{3,0},{4,5},{5,6},{6,7},{7,4},{8,9},{9,10},{10,1... | collective-permute-start | bytes 196616 | tf_op jit(solution)/shard_map/ppermute | solution.py:34
  76.3 7.0 %collective-permute-start.5 = (f32[8,8,2,128]{3,1,2,0:T(8,128)S(1)}, f32[8,8,2,128]{3,1,2,0:T(8,128)S(1)}, u32[]{:S(2)}, u32[]{:S(2)}) collective-permute-start(f32[8,8,2,128]{3,1,2,0:T(8,128)S(1)} %copy.649), channel_id=1, source_target_pairs={{1,0},{2,1},{3,2},{0,3},{5,4},{6,5},{7,6},{4,7},{9,8},{10,9},{11,1... | collective-permute-start | bytes 196616 | tf_op jit(solution)/shard_map/ppermute | solution.py:35
  81.3 1.0 %copy-start.4 = (f32[8,8,16,128]{3,2,1,0:T(8,128)S(1)}, f32[8,8,16,128]{3,2,1,0:T(8,128)}, u32[]{:S(2)}) copy-start(f32[8,8,16,128]{3,2,1,0:T(8,128)} %constant_dynamic-update-slice_fusion.61) | copy-start | bytes 1572868
  83.7 9.1 %collective-permute-start.6 = (f32[8,2,20,128]{3,0,2,1:T(8,128)S(1)}, f32[8,2,20,128]{3,0,2,1:T(8,128)S(1)}, u32[]{:S(2)}, u32[]{:S(2)}) collective-permute-start(f32[8,2,20,128]{3,0,2,1:T(8,128)S(1)} %copy.654), channel_id=1, source_target_pairs={{0,4},{4,8},{8,12},{12,16},{16,20},{20,24},{24,28},{1,5},{5,9},{9,... | collective-permute-start | bytes 491528 | tf_op jit(solution)/shard_map/ppermute | solution.py:34
  87.4 8.8 %collective-permute-start.7 = (f32[8,2,20,128]{3,0,2,1:T(8,128)S(1)}, f32[8,2,20,128]{3,0,2,1:T(8,128)S(1)}, u32[]{:S(2)}, u32[]{:S(2)}) collective-permute-start(f32[8,2,20,128]{3,0,2,1:T(8,128)S(1)} %copy.658), channel_id=1, source_target_pairs={{4,0},{8,4},{12,8},{16,12},{20,16},{24,20},{28,24},{5,1},{9,5},{13... | collective-permute-start | bytes 491528 | tf_op jit(solution)/shard_map/ppermute | solution.py:35
